TPU v7x, 256 devices: a whole 4x4x8 slice. The times are simulated.
256 devices in a mesh: farcp: 8 (over z), nearcp: 4 (over x), tp: 8 (over y, core).
Axes of the slice: x: 4, y: 4, z: 8, core: 2. Of those that a mesh axis runs over, the one named last changes fastest.
Arguments:
- raw_keys: bfloat16 [32, 16384, 8, 128], P(None, ('farcp', 'nearcp'), 'tp'), may hold values from -6 to 6
- raw_values: bfloat16 [32, 16384, 8, 128], P(None, ('farcp', 'nearcp'), 'tp'), may hold values from -6 to 6
- turn_angle: float32 [16384, 64], replicated, may hold values from -3.140625 to 3.140625
Outputs:
- stored_keys: bfloat16 [32, 16384, 8, 128], P(('farcp', 'nearcp'), None, 'tp')
- stored_values: bfloat16 [32, 16384, 8, 128], P(('farcp', 'nearcp'), None, 'tp')
- key_scale: float32 [32, 8, 128], P(('farcp', 'nearcp'), 'tp')
All inputs are finite; a program needn't handle non-finite values. Where the computation divides by a largest or mean magnitude, that divisor is 1e-20 or more.
Results may differ from a plain program's by a relative error of at most 0.001.
Values may be sent and summed in bfloat16 or wider, within the bound.
A program may use at most 128 MiB of HBM per device.

v0:
```python
import jax
import jax.numpy as jnp
from jax import lax
from jax.sharding import PartitionSpec as P


def side_by_side(arrays, axis, split_dim, concat_dim, along):
    both = jnp.concatenate(arrays, axis=along)
    result, at, done = (
        lax.all_to_all(both, axis, split_axis=split_dim, concat_axis=concat_dim, tiled=True),
        0,
        [],
    )
    for a in arrays:
        done.append(lax.slice_in_dim(result, at, at + a.shape[along], axis=along))
        at += a.shape[along]
    return tuple(done)


def turn_pairs(vectors, angle):
    half = vectors.shape[-1] // 2
    cosine, sine = (jnp.cos(angle)[None, :, None, :], jnp.sin(angle)[None, :, None, :])
    first, second = (vectors[..., :half], vectors[..., half:])
    return jnp.concatenate(
        [first * cosine - second * sine, second * cosine + first * sine], axis=-1
    )


def ready_to_store(plain_keys, angle):
    wide_keys = plain_keys.astype(jnp.float32)
    return turn_pairs(wide_keys, angle)


def body(raw_keys, raw_values, turn_angle):
    moved_keys, stored_values = side_by_side((raw_keys, raw_values), ("farcp", "nearcp"), 0, 1, 2)
    turned_keys = ready_to_store(moved_keys, turn_angle)
    key_scale = jnp.max(jnp.abs(turned_keys), axis=1)
    narrow_keys = (turned_keys / key_scale[:, None]).astype(jnp.bfloat16)
    return (narrow_keys, stored_values, key_scale)


def solution(mesh):
    placed = (
        P(None, ("farcp", "nearcp"), "tp", None),
        P(None, ("farcp", "nearcp"), "tp", None),
        P(),
    )
    return jax.shard_map(
        body,
        mesh=mesh,
        in_specs=placed,
        out_specs=(
            P(("farcp", "nearcp"), None, "tp", None),
            P(("farcp", "nearcp"), None, "tp", None),
            P(("farcp", "nearcp"), "tp", None),
        ),
        check_vma=False,
    )
```

profile of v0, /device:TPU:2, one launch (start us, length us, event | category | flops | bytes accessed | tf_op | source)
XLA Modules:
  0.0 256.5 jit_solution(15198878966169068561)
XLA Ops:
  0.6 7.5 %pad_maximum_fusion = bf16[32,512,2,128]{3,1,2,0:T(8,128)(2,1)} fusion(bf16[32,512,1,128]{3,1,2,0:T(8,128)(2,1)} %param.4, bf16[32,512,1,128]{3,1,2,0:T(8,128)(2,1)} %param.3), kind=kLoop, calls=%fused_computation | loop fusion | flops 4194304 | bytes 16777216 | tf_op jit(solution)/shard_map/concatenate | solution.py:8
  8.1 11.7 %all-to-all-start = ((bf16[32,512,2,128]{3,1,2,0:T(8,128)(2,1)}), bf16[32,512,2,128]{3,1,2,0:T(8,128)(2,1)}, u32[]{:S(2)}, u32[]{:S(2)}) async-start(bf16[32,512,2,128]{3,1,2,0:T(8,128)(2,1)} %pad_maximum_fusion), calls=%async_computation | async-start | bytes 16777216 | tf_op jit(solution)/shard_map/all_to_all | solution.py:10
  19.8 6.9 %copy.7 = f32[16384,64]{1,0:T(8,128)} copy(f32[16384,64]{0,1:T(8,128)} %param.5) | data formatting | bytes 8388608 | tf_op args[2]
  26.7 31.5 %fusion.3 = (f32[16384,64]{1,0:T(8,128)}, f32[16384,64]{1,0:T(8,128)}) fusion(f32[16384,64]{1,0:T(8,128)} %copy.7), kind=kLoop, calls=%fused_computation.12 | loop fusion | bytes 12582912 | tf_op jit(solution)/shard_map/cos | solution.py:22
  58.2 151.9 %all-to-all-done = bf16[32,512,2,128]{3,1,2,0:T(8,128)(2,1)} async-done(((bf16[32,512,2,128]{3,1,2,0:T(8,128)(2,1)}), bf16[32,512,2,128]{3,1,2,0:T(8,128)(2,1)}, u32[]{:S(2)}, u32[]{:S(2)}) %all-to-all-start) | async-done | bytes 8388640 | tf_op jit(solution)/shard_map/all_to_all | solution.py:10
  210.1 7.6 %copy.6 = bf16[32,512,2,128]{3,1,0,2:T(8,128)(2,1)} copy(bf16[32,512,2,128]{3,1,2,0:T(8,128)(2,1)} %all-to-all-done) | data formatting | bytes 16777216 | tf_op jit(solution)/shard_map/all_to_all | solution.py:10
  217.7 7.3 %fusion.2 = (bf16[1,16384,1,128]{3,1,2,0:T(8,128)(2,1)}, f32[1,16384,1,128]{3,1,2,0:T(8,128)}) fusion(bf16[1,16384,2,128]{3,1,2,0:T(8,128)(2,1)} %bitcast.16), kind=kLoop, calls=%fused_computation.11 | loop fusion | flops 2097152 | bytes 20971520 | tf_op jit(solution)/shard_map/slice | solution.py:15
  225.0 17.3 %fusion = (f32[1,16384,1,64]{3,1,2,0:T(8,128)}, f32[1,16384,1,64]{3,1,2,0:T(8,128)}) fusion(f32[16384,64]{1,0:T(8,128)} %get-tuple-element.8, f32[16384,64]{1,0:T(8,128)} %get-tuple-element.7, f32[1,16384,1,128]{3,1,2,0:T(8,128)} %get-tuple-element.6), kind=kLoop, calls=%fused_computation.4 | loop fusion | flops 6291456 | bytes 25165824 | tf_op jit(solution)/shard_map/sub | solution.py:25
  242.3 0.0 copy-start
  242.3 0.0 copy-start.1
  242.3 7.7 %abs_reduce_fusion = f32[128]{0:T(128)S(1)} fusion(f32[1,16384,1,64]{3,1,2,0:T(8,128)} %get-tuple-element.4, f32[1,16384,1,64]{3,1,2,0:T(8,128)} %get-tuple-element.3), kind=kLoop, calls=%fused_computation.9 | loop fusion | flops 6291328 | bytes 8389120 | tf_op jit(solution)/shard_map/reduce_max | solution.py:37
  250.0 0.6 copy-done
  250.5 2.4 copy-done.1
  252.9 0.0 copy-start.2
  252.9 3.6 %divide_convert_fusion = bf16[1,16384,1,128]{3,1,2,0:T(8,128)(2,1)} fusion(f32[128]{0:T(128)S(1)} %abs_reduce_fusion, f32[1,16384,1,64]{3,1,2,0:T(8,128)S(1)} %copy-done.1, f32[1,16384,1,64]{3,1,2,0:T(8,128)S(1)} %copy-done), kind=kLoop, calls=%fused_computation.8 | loop fusion | flops 6291456 | bytes 12583424 | tf_op jit(solution)/shard_map/convert_element_type | solution.py:38
  256.5 0.0 copy-done.2
Async XLA Ops:
  8.1 202.0 %all-to-all-start = ((bf16[32,512,2,128]{3,1,2,0:T(8,128)(2,1)}), bf16[32,512,2,128]{3,1,2,0:T(8,128)(2,1)}, u32[]{:S(2)}, u32[]{:S(2)}) async-start(bf16[32,512,2,128]{3,1,2,0:T(8,128)(2,1)} %pad_maximum_fusion), calls=%async_computation | async-start | bytes 16777216 | tf_op jit(solution)/shard_map/all_to_all | solution.py:10
  242.3 8.2 %copy-start = (f32[1,16384,1,64]{3,1,2,0:T(8,128)S(1)}, f32[1,16384,1,64]{3,1,2,0:T(8,128)}, u32[]{:S(2)}) copy-start(f32[1,16384,1,64]{3,1,2,0:T(8,128)} %get-tuple-element.3) | copy-start | bytes 12582916
  242.3 10.6 %copy-start.1 = (f32[1,16384,1,64]{3,1,2,0:T(8,128)S(1)}, f32[1,16384,1,64]{3,1,2,0:T(8,128)}, u32[]{:S(2)}) copy-start(f32[1,16384,1,64]{3,1,2,0:T(8,128)} %get-tuple-element.4) | copy-start | bytes 12582916
  252.9 3.6 %copy-start.2 = (f32[128]{0:T(128)}, f32[128]{0:T(128)S(1)}, u32[]{:S(2)}) copy-start(f32[128]{0:T(128)S(1)} %abs_reduce_fusion) | copy-start | bytes 1540
where the time goes:
time: 261 us; the launch traced here: 257 us
  waiting for transfers between devices  152 us (58%)
  local copies, waits for them, and re-layouts  49 us (19%)
  other arithmetic  43.3 us (17%)
  starting transfers between devices  11.7 us (4%)
    all_to_all x1, waiting for transfers between devices, side_by_side(): lax.all_to_all(both, axis, split_axis=split_dim, concat_axis=concat_dim,...  152 us
    cos x1, local copies, waits for them, and re-layouts, turn_pairs(): jnp.cos(angle)[None, :, None, :]  31.5 us
    sub x1, other arithmetic, turn_pairs(): first * cosine - second * sine  17.3 us
    all_to_all x1, starting transfers between devices, side_by_side(): lax.all_to_all(both, axis, split_axis=split_dim, concat_axis=concat_dim,...  11.7 us
    unnamed x7, local copies, waits for them, and re-layouts  9.82 us
    reduce_max x1, other arithmetic, body(): key_scale = jnp.max(jnp.abs(turned_keys), axis=1)  7.65 us
    all_to_all x1, local copies, waits for them, and re-layouts, side_by_side(): lax.all_to_all(both, axis, split_axis=split_dim, concat_axis=concat_dim,...  7.6 us
    concatenate x1, other arithmetic, side_by_side(): both = jnp.concatenate(arrays, axis=along)  7.47 us
  transfers between devices with their start and end apart: 1, of which 1 were waited for; matrix products, arithmetic and copies ran while one was open for 15% of the time, Pallas kernels for 0%

commit v1 on v0

v1 whole, which is shorter than its diff:
```python
import functools

import jax
import jax.numpy as jnp
from jax import lax
from jax.experimental import pallas as pl
from jax.experimental.pallas import tpu as pltpu
from jax.sharding import PartitionSpec as P

MESH = pl.DeviceIdType.MESH
AX = ("farcp", "nearcp")


def ring(d, n):
    return min(d % n, n - d % n)


def exchange(nf, nn, rows, half, keys, values, angle, narrow, moved, scale, landed, table_c, table_s, angles,
             key_send, key_recv, val_send, val_recv, own_sem, angle_sem):
    far, near = lax.axis_index("farcp"), lax.axis_index("nearcp")
    me = far * nn + near
    n = nf * nn
    steps = [(a, b) for a in range(nf) for b in range(nn) if (a, b) != (0, 0)]
    steps.sort(key=lambda s: (ring(s[0], nf), ring(s[1], nn)))

    def peer(step):
        return lax.rem(far + step[0], nf), lax.rem(near + step[1], nn)

    def block(index):
        return pl.ds(pl.multiple_of(index * rows, rows), rows)

    barrier = pltpu.get_barrier_semaphore()
    for step in steps:
        f, x = peer(step)
        pl.semaphore_signal(barrier, inc=1, device_id={"farcp": f, "nearcp": x}, device_id_type=MESH)
    own = [
        pltpu.make_async_copy(keys.at[me], landed.at[block(me)], own_sem.at[0]),
        pltpu.make_async_copy(values.at[me], moved.at[block(me)], own_sem.at[1]),
        pltpu.make_async_copy(angle, angles, angle_sem),
    ]
    for copy in own:
        copy.start()
    pl.semaphore_wait(barrier, n - 1)

    for source, target, send, recv in ((keys, landed, key_send, key_recv), (values, moved, val_send, val_recv)):
        for step in steps:
            f, x = peer(step)
            pltpu.make_async_remote_copy(
                source.at[f * nn + x], target.at[block(me)], send, recv,
                device_id={"farcp": f, "nearcp": x}, device_id_type=MESH,
            ).start()

    own[2].wait()

    def tables(i, carry):
        a = angles[:, block(i)]
        c, s = jnp.cos(a), jnp.sin(a)
        table_c[block(i), :] = jnp.concatenate([c, c], axis=0).T
        table_s[block(i), :] = jnp.concatenate([-s, s], axis=0).T
        return carry

    lax.fori_loop(0, n, tables, 0)

    def wait_all(ref, sem):
        part = ref.at[pl.ds(0, (n - 1) * rows)]
        pltpu.make_async_copy(part, part, sem).wait()

    own[0].wait()
    wait_all(landed, key_recv)

    def turn(i, largest):
        k = landed[block(i), :].astype(jnp.float32)
        t = k * table_c[block(i), :] + pltpu.roll(k, half, 1) * table_s[block(i), :]
        table_c[block(i), :] = t
        return jnp.maximum(largest, jnp.max(jnp.abs(t).reshape(rows // 8, 8, 2 * half), axis=0))

    largest = lax.fori_loop(0, n, turn, jnp.zeros((8, 2 * half), jnp.float32))
    top = jnp.max(largest, axis=0, keepdims=True)
    scale[...] = top

    def narrower(i, carry):
        narrow[block(i), :] = (table_c[block(i), :] / top).astype(jnp.bfloat16)
        return carry

    lax.fori_loop(0, n, narrower, 0)

    own[1].wait()
    wait_all(moved, val_recv)
    wait_all(landed, key_send)
    wait_all(moved, val_send)


def flush(narrow, moved, scale, narrow_out, moved_out, scale_out, sems):
    scale_out[...] = scale[...]
    n = 8
    rows = narrow.shape[0] // n
    copies = []
    for i in range(n):
        part = pl.ds(i * rows, rows)
        copies.append(pltpu.make_async_copy(narrow.at[part], narrow_out.at[part], sems.at[2 * i]))
        copies.append(pltpu.make_async_copy(moved.at[part], moved_out.at[part], sems.at[2 * i + 1]))
    for c in copies:
        c.start()
    for c in copies:
        c.wait()


def solution(mesh):
    nf, nn = mesh.shape["farcp"], mesh.shape["nearcp"]
    n = nf * nn

    def body(raw_keys, raw_values, turn_angle):
        batch, rows, _, size = raw_keys.shape
        length = rows * n
        keys = pltpu.with_memory_space_constraint(raw_keys.reshape(batch, rows, size), pltpu.HBM)
        values = pltpu.with_memory_space_constraint(raw_values.reshape(batch, rows, size), pltpu.HBM)
        angle = pltpu.with_memory_space_constraint(turn_angle.T, pltpu.HBM)
        wide = jax.ShapeDtypeStruct((length, size), jnp.bfloat16)
        small = jax.ShapeDtypeStruct((1, size), jnp.float32)
        hbm = pl.BlockSpec(memory_space=pltpu.HBM)
        vmem = pl.BlockSpec(memory_space=pltpu.VMEM)
        dma = pltpu.SemaphoreType.DMA
        narrow, moved, scale = pl.pallas_call(
            functools.partial(exchange, nf, nn, rows, size // 2),
            name="exchange",
            out_shape=(wide, wide, small),
            in_specs=[hbm] * 3,
            out_specs=(vmem, vmem, vmem),
            scratch_shapes=[
                pltpu.VMEM((length, size), jnp.bfloat16),
                pltpu.VMEM((length, size), jnp.float32),
                pltpu.VMEM((length, size), jnp.float32),
                pltpu.VMEM((size // 2, length), jnp.float32),
                dma, dma, dma, dma, dma((2,)), dma,
            ],
            compiler_params=pltpu.CompilerParams(
                collective_id=0, has_side_effects=True, vmem_limit_bytes=36 * 2**20
            ),
        )(keys, values, angle)
        stored_keys, stored_values, key_scale = pl.pallas_call(
            flush,
            name="flush",
            out_shape=(wide, wide, small),
            in_specs=[vmem, vmem, vmem],
            out_specs=(hbm, hbm, vmem),
            scratch_shapes=[dma((16,))],
            compiler_params=pltpu.CompilerParams(vmem_limit_bytes=4 * 2**20),
        )(narrow, moved, scale)
        return (
            stored_keys.reshape(1, length, 1, size),
            stored_values.reshape(1, length, 1, size),
            key_scale.reshape(1, 1, size),
        )

    return jax.shard_map(
        body, mesh=mesh,
        in_specs=(P(None, AX, "tp", None), P(None, AX, "tp", None), P()),
        out_specs=(P(AX, None, "tp", None), P(AX, None, "tp", None), P(AX, "tp", None)),
        check_vma=False,
    )
```

time: 261 us -> 202 us (0.77); the launches traced: 257 us -> 202 us
  Pallas kernels: 0 us -> 201 us
  waiting for transfers between devices: 152 us -> 0 us
  local copies, waits for them, and re-layouts: 49 us -> 0 us
  other arithmetic: 43.3 us -> 0 us
  starting transfers between devices: 11.7 us -> 0 us
    pallas_call x0 -> x2, Pallas kernels: none -> 201 us  [the longest x1 198 us: body(): pl.pallas_call(functools.partial(exchange, nf, nn, rows, size // 2), name...]
    all_to_all x1 -> x0, waiting for transfers between devices: 152 us -> none  [side_by_side(): lax.all_to_all(both, axis, split_axis=split_dim, concat_axis=concat_dim,...]
    cos x1 -> x0, local copies, waits for them, and re-layouts: 31.5 us -> none  [turn_pairs(): jnp.cos(angle)[None, :, None, :]]
    sub x1 -> x0, other arithmetic: 17.3 us -> none  [turn_pairs(): first * cosine - second * sine]
    all_to_all x1 -> x0, starting transfers between devices: 11.7 us -> none  [side_by_side(): lax.all_to_all(both, axis, split_axis=split_dim, concat_axis=concat_dim,...]
    unnamed x7 -> x0, local copies, waits for them, and re-layouts: 9.82 us -> none
    reduce_max x1 -> x0, other arithmetic: 7.65 us -> none  [body(): key_scale = jnp.max(jnp.abs(turned_keys), axis=1)]
    all_to_all x1 -> x0, local copies, waits for them, and re-layouts: 7.6 us -> none  [side_by_side(): lax.all_to_all(both, axis, split_axis=split_dim, concat_axis=concat_dim,...]
  transfers between devices with their start and end apart: 1 -> 0, of which waited for: 1 -> 0; matrix products, arithmetic and copies ran while one was open for 15% -> 0% of each run, Pallas kernels for 0% -> 0%
where the time goes in v1:
time: 202 us
  Pallas kernels  201 us (100%)
    pallas_call x1, Pallas kernels, body(): pl.pallas_call(functools.partial(exchange, nf, nn, rows, size // 2), name...  198 us

profile of v1, /device:TPU:2, one launch (start us, length us, event | category | flops | bytes accessed | tf_op | source)
XLA Modules:
  0.0 202.1 jit_solution(10955526423724286193)
XLA Ops:
  0.6 197.5 %exchange.1 = (bf16[16384,128]{1,0:T(8,128)(2,1)S(1)}, bf16[16384,128]{1,0:T(8,128)(2,1)S(1)}, f32[1,128]{1,0:T(1,128)S(1)}) custom-call(bf16[32,512,128]{2,1,0:T(8,128)(2,1)} %bitcast.6, bf16[32,512,128]{2,1,0:T(8,128)(2,1)} %bitcast.7, f32[64,16384]{1,0:T(8,128)} %bitcast.8), custom_call_target="tpu_custom_call" | custom-call | tf_op jit(solution)/shard_map/exchange/pallas_call | solution.py:123
  198.2 3.9 %flush.1 = (bf16[16384,128]{1,0:T(8,128)(2,1)}, bf16[16384,128]{1,0:T(8,128)(2,1)}, f32[1,128]{1,0:T(1,128)}) custom-call(bf16[16384,128]{1,0:T(8,128)(2,1)S(1)} %get-tuple-element.9.narrow, bf16[16384,128]{1,0:T(8,128)(2,1)S(1)} %get-tuple-element.10.moved, f32[1,128]{1,0:T(1,128)S(1)} %get-tuple-element.11.scale), custom_call_target="tpu_custom_call" | custom-call | tf_op jit(solution)/shard_map/flush/pallas_call | solution.py:140

commit v2 on v1

--- a/solution.py
+++ b/solution.py
@@ -9,28 +9,43 @@
 
 MESH = pl.DeviceIdType.MESH
 AX = ("farcp", "nearcp")
+PARTS = 2
+NEXT = ((1, 0), (-1, 0), (0, 1), (0, -1))
 
 
 def ring(d, n):
     return min(d % n, n - d % n)
 
 
+def peers(nf, nn):
+    pattern = [(1, 1), (-1, -1), (-1, 1), (1, -1), (1, 0), (-1, 0), (1, 2), (-1, 2)]
+    order = [(sign * c % nf, b % nn) for c in [*range(1, nf // 2 + 1), 0] for sign, b in pattern]
+    return [s for s in dict.fromkeys(order) if s != (0, 0)]
+
+
 def exchange(nf, nn, rows, half, keys, values, angle, narrow, moved, scale, landed, table_c, table_s, angles,
-             key_send, key_recv, val_send, val_recv, own_sem, angle_sem):
+             key_send, key_recv, val_send, val_recv, own_sem, angle_sem, entered):
     far, near = lax.axis_index("farcp"), lax.axis_index("nearcp")
     me = far * nn + near
     n = nf * nn
-    steps = [(a, b) for a in range(nf) for b in range(nn) if (a, b) != (0, 0)]
-    steps.sort(key=lambda s: (ring(s[0], nf), ring(s[1], nn)))
+    steps = peers(nf, nn)
 
     def peer(step):
-        return lax.rem(far + step[0], nf), lax.rem(near + step[1], nn)
+        return lax.rem(far + step[0] % nf, nf), lax.rem(near + step[1] % nn, nn)
 
     def block(index):
         return pl.ds(pl.multiple_of(index * rows, rows), rows)
 
+    def start(source, target, send, recv, step, p):
+        f, x = peer(step)
+        here = pl.ds(pl.multiple_of(me * rows + p * part, part), part)
+        pltpu.make_async_remote_copy(
+            source.at[f * nn + x, pl.ds(p * part, part)], target.at[here], send, recv,
+            device_id={"farcp": f, "nearcp": x}, device_id_type=MESH,
+        ).start()
+
     barrier = pltpu.get_barrier_semaphore()
-    for step in steps:
+    for step in NEXT:
         f, x = peer(step)
         pl.semaphore_signal(barrier, inc=1, device_id={"farcp": f, "nearcp": x}, device_id_type=MESH)
     own = [
@@ -40,15 +55,27 @@
     ]
     for copy in own:
         copy.start()
-    pl.semaphore_wait(barrier, n - 1)
+    pl.semaphore_wait(barrier, len(NEXT))
 
-    for source, target, send, recv in ((keys, landed, key_send, key_recv), (values, moved, val_send, val_recv)):
+    part = rows // PARTS
+    hops = nf // 2 + nn // 2
+    for distance in range(1, hops + 1):
+        if distance > 1:
+            for i in range(len(NEXT)):
+                pl.semaphore_wait(entered.at[i], 1)
+        if distance < hops:
+            for i, step in enumerate(NEXT):
+                f, x = peer(step)
+                pl.semaphore_signal(entered.at[i], inc=1, device_id={"farcp": f, "nearcp": x}, device_id_type=MESH)
         for step in steps:
-            f, x = peer(step)
-            pltpu.make_async_remote_copy(
-                source.at[f * nn + x], target.at[block(me)], send, recv,
-                device_id={"farcp": f, "nearcp": x}, device_id_type=MESH,
-            ).start()
+            if ring(step[0], nf) + ring(step[1], nn) == distance:
+                start(keys, landed, key_send, key_recv, step, 0)
+    for p in range(1, PARTS):
+        for step in steps:
+            start(keys, landed, key_send, key_recv, step, p)
+    for p in range(PARTS):
+        for step in steps:
+            start(values, moved, val_send, val_recv, step, p)
 
     own[2].wait()
 
@@ -91,18 +118,17 @@
 
 
 def flush(narrow, moved, scale, narrow_out, moved_out, scale_out, sems):
-    scale_out[...] = scale[...]
-    n = 8
-    rows = narrow.shape[0] // n
-    copies = []
-    for i in range(n):
+    pieces = 8
+    rows = narrow.shape[0] // pieces
+    copies = [pltpu.make_async_copy(scale, scale_out, sems.at[2 * pieces])]
+    for i in range(pieces):
         part = pl.ds(i * rows, rows)
         copies.append(pltpu.make_async_copy(narrow.at[part], narrow_out.at[part], sems.at[2 * i]))
         copies.append(pltpu.make_async_copy(moved.at[part], moved_out.at[part], sems.at[2 * i + 1]))
-    for c in copies:
-        c.start()
-    for c in copies:
-        c.wait()
+    for copy in copies:
+        copy.start()
+    for copy in copies:
+        copy.wait()
 
 
 def solution(mesh):
@@ -132,6 +158,7 @@
                 pltpu.VMEM((length, size), jnp.float32),
                 pltpu.VMEM((size // 2, length), jnp.float32),
                 dma, dma, dma, dma, dma((2,)), dma,
+                pltpu.SemaphoreType.REGULAR((len(NEXT),)),
             ],
             compiler_params=pltpu.CompilerParams(
                 collective_id=0, has_side_effects=True, vmem_limit_bytes=36 * 2**20
@@ -142,8 +169,8 @@
             name="flush",
             out_shape=(wide, wide, small),
             in_specs=[vmem, vmem, vmem],
-            out_specs=(hbm, hbm, vmem),
-            scratch_shapes=[dma((16,))],
+            out_specs=(hbm, hbm, hbm),
+            scratch_shapes=[dma((17,))],
             compiler_params=pltpu.CompilerParams(vmem_limit_bytes=4 * 2**20),
         )(narrow, moved, scale)
         return (

time: 202 us -> 195 us (0.965)
  Pallas kernels: 201 us -> 194 us
    pallas_call x1, Pallas kernels: 198 us -> 190 us  [body(): pl.pallas_call(functools.partial(exchange, nf, nn, rows, size // 2), name...]
where the time goes in v2:
time: 195 us
  Pallas kernels  194 us (99%)
    pallas_call x1, Pallas kernels, body(): pl.pallas_call(functools.partial(exchange, nf, nn, rows, size // 2), name...  190 us

profile of v2, /device:TPU:2, one launch (start us, length us, event | category | flops | bytes accessed | tf_op | source)
XLA Modules:
  0.0 194.5 jit_solution(7508920522272302808)
XLA Ops:
  0.6 190.5 %exchange.1 = (bf16[16384,128]{1,0:T(8,128)(2,1)S(1)}, bf16[16384,128]{1,0:T(8,128)(2,1)S(1)}, f32[1,128]{1,0:T(1,128)S(1)}) custom-call(bf16[32,512,128]{2,1,0:T(8,128)(2,1)} %bitcast.6, bf16[32,512,128]{2,1,0:T(8,128)(2,1)} %bitcast.7, f32[64,16384]{1,0:T(8,128)} %bitcast.8), custom_call_target="tpu_custom_call" | custom-call | tf_op jit(solution)/shard_map/exchange/pallas_call | solution.py:149
  191.1 3.4 %flush.1 = (bf16[16384,128]{1,0:T(8,128)(2,1)}, bf16[16384,128]{1,0:T(8,128)(2,1)}, f32[1,128]{1,0:T(1,128)}) custom-call(bf16[16384,128]{1,0:T(8,128)(2,1)S(1)} %get-tuple-element.9.narrow, bf16[16384,128]{1,0:T(8,128)(2,1)S(1)} %get-tuple-element.10.moved, f32[1,128]{1,0:T(1,128)S(1)} %get-tuple-element.11.scale), custom_call_target="tpu_custom_call" | custom-call | tf_op jit(solution)/shard_map/flush/pallas_call | solution.py:167

commit v3 on v2

--- a/solution.py
+++ b/solution.py
@@ -9,8 +9,8 @@
 
 MESH = pl.DeviceIdType.MESH
 AX = ("farcp", "nearcp")
-PARTS = 2
 NEXT = ((1, 0), (-1, 0), (0, 1), (0, -1))
+PASSES = 4
 
 
 def ring(d, n):
@@ -23,12 +23,19 @@
     return [s for s in dict.fromkeys(order) if s != (0, 0)]
 
 
-def exchange(nf, nn, rows, half, keys, values, angle, narrow, moved, scale, landed, table_c, table_s, angles,
-             key_send, key_recv, val_send, val_recv, own_sem, angle_sem, entered):
+def deadlines(nf, nn):
+    far = [*range(nf // 2), nf - 1, *range(nf // 2, nf - 1)]
+    near = [*range(nn - 2), nn - 1, nn - 2]
+    return [(f, x) for f in far for x in near]
+
+
+def exchange(nf, nn, rows, half, keys, values, angle, narrow, moved, scale, landed, table_c, table_s, angles, first,
+             key_send, key_recv, val_send, val_recv, own_sem, angle_sem, first_sem, entered):
     far, near = lax.axis_index("farcp"), lax.axis_index("nearcp")
     me = far * nn + near
     n = nf * nn
     steps = peers(nf, nn)
+    middle = rows // 2
 
     def peer(step):
         return lax.rem(far + step[0] % nf, nf), lax.rem(near + step[1] % nn, nn)
@@ -36,46 +43,59 @@
     def block(index):
         return pl.ds(pl.multiple_of(index * rows, rows), rows)
 
-    def start(source, target, send, recv, step, p):
-        f, x = peer(step)
-        here = pl.ds(pl.multiple_of(me * rows + p * part, part), part)
+    def push(source, target, send, recv, f, x):
         pltpu.make_async_remote_copy(
-            source.at[f * nn + x, pl.ds(p * part, part)], target.at[here], send, recv,
-            device_id={"farcp": f, "nearcp": x}, device_id_type=MESH,
+            source, target, send, recv, device_id={"farcp": f, "nearcp": x}, device_id_type=MESH
         ).start()
+
+    def here(at, size):
+        return pl.ds(pl.multiple_of(me * rows + at, size), size)
+
+    def push_keys(f, x, at, size):
+        push(keys.at[f * nn + x, pl.ds(at, size)], landed.at[here(at, size)], key_send, key_recv, f, x)
+
+    def push_values(f, x, at, size):
+        push(values.at[f * nn + x, pl.ds(at, size)], moved.at[here(at, size)], val_send, val_recv, f, x)
 
     barrier = pltpu.get_barrier_semaphore()
     for step in NEXT:
         f, x = peer(step)
         pl.semaphore_signal(barrier, inc=1, device_id={"farcp": f, "nearcp": x}, device_id_type=MESH)
+    early = []
+    for i, step in enumerate(NEXT):
+        f, x = peer(step)
+        early.append(pltpu.make_async_copy(keys.at[f * nn + x], first.at[i], first_sem.at[i]))
     own = [
         pltpu.make_async_copy(keys.at[me], landed.at[block(me)], own_sem.at[0]),
         pltpu.make_async_copy(values.at[me], moved.at[block(me)], own_sem.at[1]),
         pltpu.make_async_copy(angle, angles, angle_sem),
     ]
-    for copy in own:
+    for copy in early + own:
         copy.start()
     pl.semaphore_wait(barrier, len(NEXT))
-
-    part = rows // PARTS
-    hops = nf // 2 + nn // 2
-    for distance in range(1, hops + 1):
-        if distance > 1:
-            for i in range(len(NEXT)):
-                pl.semaphore_wait(entered.at[i], 1)
-        if distance < hops:
-            for i, step in enumerate(NEXT):
-                f, x = peer(step)
-                pl.semaphore_signal(entered.at[i], inc=1, device_id={"farcp": f, "nearcp": x}, device_id_type=MESH)
+    for i, step in enumerate(NEXT):
+        early[i].wait()
+        push(first.at[i], landed.at[block(me)], key_send, key_recv, *peer(step))
+
+    for distance in range(2, nf // 2 + nn // 2 + 1):
+        for i, step in enumerate(NEXT):
+            f, x = peer(step)
+            pl.semaphore_signal(entered.at[i], inc=1, device_id={"farcp": f, "nearcp": x}, device_id_type=MESH)
+        for i in range(len(NEXT)):
+            pl.semaphore_wait(entered.at[i], 1)
         for step in steps:
             if ring(step[0], nf) + ring(step[1], nn) == distance:
-                start(keys, landed, key_send, key_recv, step, 0)
-    for p in range(1, PARTS):
-        for step in steps:
-            start(keys, landed, key_send, key_recv, step, p)
-    for p in range(PARTS):
-        for step in steps:
-            start(values, moved, val_send, val_recv, step, p)
+                push_keys(*peer(step), 0, middle)
+
+    for step in steps:
+        if ring(step[0], nf) + ring(step[1], nn) > 1:
+            push_keys(*peer(step), middle, middle)
+    for step in steps:
+        push_values(*peer(step), 0, middle)
+    size = middle // PASSES
+    for p in range(PASSES):
+        for f, x in deadlines(nf, nn):
+            pl.when((far != f) | (near != x))(functools.partial(push_values, f, x, middle + p * size, size))
 
     own[2].wait()
 
@@ -118,7 +138,7 @@
 
 
 def flush(narrow, moved, scale, narrow_out, moved_out, scale_out, sems):
-    pieces = 8
+    pieces = 4
     rows = narrow.shape[0] // pieces
     copies = [pltpu.make_async_copy(scale, scale_out, sems.at[2 * pieces])]
     for i in range(pieces):
@@ -138,9 +158,10 @@
     def body(raw_keys, raw_values, turn_angle):
         batch, rows, _, size = raw_keys.shape
         length = rows * n
-        keys = pltpu.with_memory_space_constraint(raw_keys.reshape(batch, rows, size), pltpu.HBM)
-        values = pltpu.with_memory_space_constraint(raw_values.reshape(batch, rows, size), pltpu.HBM)
-        angle = pltpu.with_memory_space_constraint(turn_angle.T, pltpu.HBM)
+        keys, values, angle = (
+            pltpu.with_memory_space_constraint(a, pltpu.HBM)
+            for a in (raw_keys.reshape(batch, rows, size), raw_values.reshape(batch, rows, size), turn_angle.T)
+        )
         wide = jax.ShapeDtypeStruct((length, size), jnp.bfloat16)
         small = jax.ShapeDtypeStruct((1, size), jnp.float32)
         hbm = pl.BlockSpec(memory_space=pltpu.HBM)
@@ -157,7 +178,8 @@
                 pltpu.VMEM((length, size), jnp.float32),
                 pltpu.VMEM((length, size), jnp.float32),
                 pltpu.VMEM((size // 2, length), jnp.float32),
-                dma, dma, dma, dma, dma((2,)), dma,
+                pltpu.VMEM((len(NEXT), rows, size), jnp.bfloat16),
+                dma, dma, dma, dma, dma((2,)), dma, dma((len(NEXT),)),
                 pltpu.SemaphoreType.REGULAR((len(NEXT),)),
             ],
             compiler_params=pltpu.CompilerParams(
@@ -170,7 +192,7 @@
             out_shape=(wide, wide, small),
             in_specs=[vmem, vmem, vmem],
             out_specs=(hbm, hbm, hbm),
-            scratch_shapes=[dma((17,))],
+            scratch_shapes=[dma((9,))],
             compiler_params=pltpu.CompilerParams(vmem_limit_bytes=4 * 2**20),
         )(narrow, moved, scale)
         return (

time: 195 us -> 192 us (0.985); the launches traced: 195 us -> 189 us
  Pallas kernels: 194 us -> 189 us
    pallas_call x1, Pallas kernels: 190 us -> 185 us  [body(): pl.pallas_call(functools.partial(exchange, nf, nn, rows, size // 2), name...]
where the time goes in v3:
time: 192 us; the launch traced here: 189 us
  Pallas kernels  189 us (98%)
    pallas_call x1, Pallas kernels, body(): pl.pallas_call(functools.partial(exchange, nf, nn, rows, size // 2), name...  185 us

profile of v3, /device:TPU:2, one launch (start us, length us, event | category | flops | bytes accessed | tf_op | source)
XLA Modules:
  0.0 189.2 jit_solution(12543800365658054279)
XLA Ops:
  0.6 185.2 %exchange.1 = (bf16[16384,128]{1,0:T(8,128)(2,1)S(1)}, bf16[16384,128]{1,0:T(8,128)(2,1)S(1)}, f32[1,128]{1,0:T(1,128)S(1)}) custom-call(bf16[32,512,128]{2,1,0:T(8,128)(2,1)} %bitcast.6, bf16[32,512,128]{2,1,0:T(8,128)(2,1)} %bitcast.7, f32[64,16384]{1,0:T(8,128)} %bitcast.8), custom_call_target="tpu_custom_call" | custom-call | tf_op jit(solution)/shard_map/exchange/pallas_call | solution.py:170
  185.8 3.4 %flush.1 = (bf16[16384,128]{1,0:T(8,128)(2,1)}, bf16[16384,128]{1,0:T(8,128)(2,1)}, f32[1,128]{1,0:T(1,128)}) custom-call(bf16[16384,128]{1,0:T(8,128)(2,1)S(1)} %get-tuple-element.9.narrow, bf16[16384,128]{1,0:T(8,128)(2,1)S(1)} %get-tuple-element.10.moved, f32[1,128]{1,0:T(1,128)S(1)} %get-tuple-element.11.scale), custom_call_target="tpu_custom_call" | custom-call | tf_op jit(solution)/shard_map/flush/pallas_call | solution.py:189

commit v4 on v3

--- a/solution.py
+++ b/solution.py
@@ -10,7 +10,7 @@
 MESH = pl.DeviceIdType.MESH
 AX = ("farcp", "nearcp")
 NEXT = ((1, 0), (-1, 0), (0, 1), (0, -1))
-PASSES = 4
+PASSES = ((1, 2), (2, 4))
 
 
 def ring(d, n):
@@ -90,12 +90,16 @@
     for step in steps:
         if ring(step[0], nf) + ring(step[1], nn) > 1:
             push_keys(*peer(step), middle, middle)
-    for step in steps:
-        push_values(*peer(step), 0, middle)
-    size = middle // PASSES
-    for p in range(PASSES):
-        for f, x in deadlines(nf, nn):
-            pl.when((far != f) | (near != x))(functools.partial(push_values, f, x, middle + p * size, size))
+    def all_values(passes):
+        at = 0
+        for size in passes:
+            for f, x in deadlines(nf, nn):
+                pl.when((far != f) | (near != x))(functools.partial(push_values, f, x, at, size))
+            at += size
+
+    for core, passes in enumerate(PASSES):
+        sizes = [middle // p for p in passes for _ in range(p)]
+        pl.when(lax.rem(lax.axis_index("tp"), 2) == core)(functools.partial(all_values, sizes))
 
     own[2].wait()
 

time: 192 us -> 192 us (level)
  no operation moved by 1% of the time
where the time goes in v4:
time: 192 us; the launch traced here: 188 us
  Pallas kernels  188 us (98%)
    pallas_call x1, Pallas kernels, body(): pl.pallas_call(functools.partial(exchange, nf, nn, rows, size // 2), name...  184 us

profile of v4, /device:TPU:2, one launch (start us, length us, event | category | flops | bytes accessed | tf_op | source)
XLA Modules:
  0.0 188.5 jit_solution(10169697907289200369)
XLA Ops:
  0.6 184.5 %exchange.1 = (bf16[16384,128]{1,0:T(8,128)(2,1)S(1)}, bf16[16384,128]{1,0:T(8,128)(2,1)S(1)}, f32[1,128]{1,0:T(1,128)S(1)}) custom-call(bf16[32,512,128]{2,1,0:T(8,128)(2,1)} %bitcast.6, bf16[32,512,128]{2,1,0:T(8,128)(2,1)} %bitcast.7, f32[64,16384]{1,0:T(8,128)} %bitcast.8), custom_call_target="tpu_custom_call" | custom-call | tf_op jit(solution)/shard_map/exchange/pallas_call | solution.py:174
  185.1 3.4 %flush.1 = (bf16[16384,128]{1,0:T(8,128)(2,1)}, bf16[16384,128]{1,0:T(8,128)(2,1)}, f32[1,128]{1,0:T(1,128)}) custom-call(bf16[16384,128]{1,0:T(8,128)(2,1)S(1)} %get-tuple-element.9.narrow, bf16[16384,128]{1,0:T(8,128)(2,1)S(1)} %get-tuple-element.10.moved, f32[1,128]{1,0:T(1,128)S(1)} %get-tuple-element.11.scale), custom_call_target="tpu_custom_call" | custom-call | tf_op jit(solution)/shard_map/flush/pallas_call | solution.py:193
